TPU v7x, 32 devices: a whole 2x2x4 slice. The times are simulated.
32 devices in a mesh: rep: 8 (over z, x), rows: 4 (over y, core).
Axes of the slice: x: 2, y: 2, z: 4, core: 2. Of those that a mesh axis runs over, the one named last changes fastest.
Arguments:
- item_table: bfloat16 [131072, 128], P(('rep', 'rows')), may hold values from -6 to 6
- history_ids: int32 [512, 64], P('rows'), may hold values from 0 to 131071, as said below
- history_mask: int32 [512, 64], P('rows'), may hold values 0 or 1
Outputs:
- user_vectors: float32 [512, 128], P('rows')
Inputs may be any that keep to these rules, and one draw needn't show every extreme that they name: `history_ids`: among the slots of the 128 bags of one index of rows (bags b * 128 to (b + 1) * 128 - 1), exactly 256 ids fall in each block of 4096 consecutive table rows, used or not.
All inputs are finite; a program needn't handle non-finite values. No bound on the sum of `history_mask` on one device may be relied on, other than what follows from the above.
Results may differ from a plain program's by a relative error of at most 0.0017.
Values may be sent and summed in bfloat16 or wider, within the bound.
No kernel may reach another device: no remote copies, remote signals or barrier semaphores. Data moves between devices by JAX's collectives and lax.ppermute only.
A program may use at most 128 MiB of HBM per device.

v0:
```python
import math
import jax
import jax.numpy as jnp
from jax import lax
from jax.sharding import PartitionSpec as P


def pool_rows(ids, mask, piece, offset):
    nbags, length = ids.shape
    block = math.gcd(nbags, 512)
    nhigh = piece.shape[0] // 128
    width = piece.shape[1]
    local = ids - offset
    high = jnp.floor_divide(local, 128)
    low = jnp.remainder(local, 128)

    def one_block(args):
        high_b, low_b, mask_b = args
        high_hot = (high_b[:, :, None] == jnp.arange(nhigh, dtype=jnp.int32)).astype(jnp.bfloat16)
        low_hot = (
            (low_b[:, :, None] == jnp.arange(128, dtype=jnp.int32)) & (mask_b[:, :, None] > 0)
        ).astype(jnp.bfloat16)
        counts = jnp.einsum("blh,blo->bho", high_hot, low_hot, preferred_element_type=jnp.float32)
        counts = counts.astype(jnp.bfloat16).reshape(block, nhigh * 128)
        return jnp.dot(counts, piece, preferred_element_type=jnp.float32)

    shaped = (
        high.reshape(-1, block, length),
        low.reshape(-1, block, length),
        mask.reshape(-1, block, length),
    )
    return lax.map(one_block, shaped).reshape(nbags, width)


def normalize(pooled):
    return pooled / jnp.sqrt(jnp.mean(pooled * pooled, axis=1, keepdims=True) + 1e-06)


def on_device(item_table, history_ids, history_mask):
    rows_dev = item_table.shape[0]
    group_size = lax.axis_size("rows")
    group_rows = rows_dev * group_size
    group_base = lax.axis_index("rep") * group_rows
    partial_value = pool_rows(
        history_ids,
        history_mask,
        lax.all_gather(item_table, "rows", axis=0, tiled=True),
        group_base,
    )
    pooled = lax.psum(partial_value, "rep")
    return normalize(pooled)


def solution(mesh):
    return jax.shard_map(
        on_device,
        mesh=mesh,
        in_specs=(P(("rep", "rows"), None), P("rows", None), P("rows", None)),
        out_specs=P("rows", None),
        check_vma=False,
    )
```

profile of v0, /device:TPU:0, one launch (start us, length us, event | category | flops | bytes accessed | tf_op | source)
XLA Modules:
  0.0 131.9 jit_solution(6185900074222709909)
XLA Ops:
  6.5 0.0 all-gather.2.cloned.1.call-start
  6.5 0.7 all-gather.2.cloned.1.call-update
  7.3 0.0 all-reduce.2.cloned.1.call-start
  7.3 0.8 add_select_fusion.1
  8.1 0.1 copy.4
  8.2 0.1 copy.5
  8.3 0.8 broadcast_compare_fusion
  9.1 0.1 copy.6
  9.2 10.8 %fusion.6 = bf16[128,128,128]{2,1,0:T(8,128)(2,1)} fusion(s32[128,64]{1,0:T(8,128)S(1)} %copy.5, s32[128,64]{1,0:T(8,128)S(1)} %copy.4, pred[128,64]{1,0:T(8,128)(4,1)S(1)} %copy.6), kind=kOutput, calls=%fused_computation.7 | convolution fusion | flops 273678336 | bytes 4268032 | tf_op jit(solution)/shard_map/while/body/eval_jaxpr/blh,blo->bho/dot_general | solution.py:23
  20.0 26.1 %all-gather.2.cloned.1.call-done = bf16[16384,128]{1,0:T(8,128)(2,1)} async-done(((bf16[4096,128]{1,0:T(8,128)(2,1)}), bf16[16384,128]{1,0:T(8,128)(2,1)}) %all-gather.2.cloned.1.call-update) | async-done | bytes 4194320 | tf_op jit(solution)/shard_map/all_gather | solution.py:47
  46.2 6.9 %fusion = f32[128,128]{1,0:T(8,128)} fusion(bf16[16384,128]{1,0:T(8,128)(2,1)} %all-gather.2.cloned.1.call-done, bf16[16,8,128,128]{3,2,1,0:T(8,128)(2,1)} %bitcast.5), kind=kOutput, calls=%fused_computation | convolution fusion | flops 536870912 | bytes 8454144 | tf_op jit(solution)/shard_map/while/body/eval_jaxpr/dot_general | solution.py:25
  53.0 0.0 all-reduce.2.cloned.1.call-update
  53.1 69.4 %all-reduce.2.cloned.1.call-done = f32[128,128]{1,0:T(8,128)} async-done(((f32[128,128]{1,0:T(8,128)}), f32[128,128]{1,0:T(8,128)}) %all-reduce.2.cloned.1.call-update) | async-done | bytes 65552 | tf_op jit(solution)/shard_map/psum | solution.py:50
  122.5 0.9 multiply_reduce_fusion
  123.5 1.6 %broadcast_divide_fusion = f32[128,128]{1,0:T(8,128)} fusion(f32[128,128]{1,0:T(8,128)} %all-reduce.2.cloned.1.call-done, f32[128]{0:T(128)S(1)} %add_sqrt_fusion), kind=kLoop, calls=%fused_computation.17 | loop fusion | flops 16384 | bytes 131584 | tf_op jit(solution)/shard_map/div | solution.py:36
  (1 shorter events, 0.0 us)
Async XLA Ops:
  6.5 39.6 %all-gather.2.cloned.1.call-start = ((), (), s32[]{:S(2)}) async-start(), calls=%async_computation | async-start | bytes 5242880 | tf_op jit(solution)/shard_map/all_gather | solution.py:47
  7.3 115.2 %all-reduce.2.cloned.1.call-start = ((), (), s32[]{:S(2)}) async-start(), calls=%async_computation.1 | async-start | bytes 131072 | tf_op jit(solution)/shard_map/psum | solution.py:50
Sparse Core Ops, SparseCore 0:
  8.9 37.2 all-gather.1
  53.2 69.2 all-reduce.1
where the time goes:
time: 132 us
  waiting for transfers between devices  96.3 us (73%)
  matrix products  17.7 us (13%)
  between operations  13.4 us (10%)
  other arithmetic  4.08 us (3%)
    psum x1, waiting for transfers between devices, on_device(): pooled = lax.psum(partial_value, 'rep')  69.4 us
    all_gather x1, waiting for transfers between devices, on_device(): lax.all_gather(item_table, 'rows', axis=0, tiled=True)  26.1 us
    dot_general x1, matrix products, one_block(): jnp.einsum('blh,blo->bho', high_hot, low_hot, preferred_element_type=jnp....  10.8 us
    dot_general x1, matrix products, one_block(): return jnp.dot(counts, piece, preferred_element_type=jnp.float32)  6.88 us
  transfers between devices with their start and end apart: 2, of which 2 were waited for; matrix products, arithmetic and copies ran while one was open for 10% of the time, Pallas kernels for 0%

commit v1 on v0

--- a/solution.py
+++ b/solution.py
@@ -47,7 +47,8 @@
         lax.all_gather(item_table, "rows", axis=0, tiled=True),
         group_base,
     )
-    pooled = lax.psum(partial_value, "rep")
+    blocks = lax.all_gather(partial_value, "rep")
+    pooled = jnp.sum(blocks, axis=0)
     return normalize(pooled)
 
 

time: 132 us -> 92 us (0.70)
  waiting for transfers between devices: 96.3 us -> 26.8 us
  blocking collectives: 0 us -> 31.6 us
  other arithmetic: 4.08 us -> 2.44 us
    psum x1 -> x0, waiting for transfers between devices: 69.4 us -> none  [on_device(): pooled = lax.psum(partial_value, 'rep')]
    all_gather x0 -> x1, blocking collectives: none -> 31.6 us  [on_device(): blocks = lax.all_gather(partial_value, 'rep')]
  transfers between devices with their start and end apart: 2 -> 1, of which waited for: 2 -> 1; matrix products, arithmetic and copies ran while one was open for 10% -> 14% of each run, Pallas kernels for 0% -> 0%
where the time goes in v1:
time: 92 us; the launch traced here: 91.7 us
  blocking collectives  31.6 us (34%)
  waiting for transfers between devices  26.8 us (29%)
  matrix products  17.1 us (19%)
  between operations  13.4 us (15%)
  other arithmetic  2.44 us (3%)
    all_gather x1, blocking collectives, on_device(): blocks = lax.all_gather(partial_value, 'rep')  31.6 us
    all_gather x1, waiting for transfers between devices, on_device(): lax.all_gather(item_table, 'rows', axis=0, tiled=True)  26.1 us
    dot_general x1, matrix products, one_block(): jnp.einsum('blh,blo->bho', high_hot, low_hot, preferred_element_type=jnp....  10.8 us
    dot_general x1, matrix products, one_block(): return jnp.dot(counts, piece, preferred_element_type=jnp.float32)  6.31 us
  transfers between devices with their start and end apart: 1, of which 1 were waited for; matrix products, arithmetic and copies ran while one was open for 14% of the time, Pallas kernels for 0%

profile of v1, /device:TPU:0, one launch (start us, length us, event | category | flops | bytes accessed | tf_op | source)
XLA Modules:
  0.0 91.7 jit_solution(13632765863746206246)
XLA Ops:
  6.5 0.0 all-gather.3.cloned.1.call-start
  6.5 0.7 all-gather.3.cloned.1.call-update
  7.3 0.8 add_select_fusion.1
  8.1 0.1 copy.4
  8.2 0.1 copy.5
  8.3 0.8 broadcast_compare_fusion
  9.0 0.1 copy.6
  9.1 10.8 %fusion.6 = bf16[128,128,128]{2,1,0:T(8,128)(2,1)} fusion(s32[128,64]{1,0:T(8,128)S(1)} %copy.5, s32[128,64]{1,0:T(8,128)S(1)} %copy.4, pred[128,64]{1,0:T(8,128)(4,1)S(1)} %copy.6), kind=kOutput, calls=%fused_computation.7 | convolution fusion | flops 273678336 | bytes 4268032 | tf_op jit(solution)/shard_map/while/body/eval_jaxpr/blh,blo->bho/dot_general | solution.py:23
  20.0 26.1 %all-gather.3.cloned.1.call-done = bf16[16384,128]{1,0:T(8,128)(2,1)} async-done(((bf16[4096,128]{1,0:T(8,128)(2,1)}), bf16[16384,128]{1,0:T(8,128)(2,1)}) %all-gather.3.cloned.1.call-update) | async-done | bytes 4194320 | tf_op jit(solution)/shard_map/all_gather | solution.py:47
  46.1 6.3 %fusion = f32[128,128]{1,0:T(8,128)S(1)} fusion(bf16[16384,128]{1,0:T(8,128)(2,1)} %all-gather.3.cloned.1.call-done, bf16[16,8,128,128]{3,2,1,0:T(8,128)(2,1)} %bitcast.7), kind=kOutput, calls=%fused_computation | convolution fusion | flops 536870912 | bytes 8454144 | tf_op jit(solution)/shard_map/while/body/eval_jaxpr/dot_general | solution.py:25
  52.4 31.6 %all-gather = f32[1024,128]{1,0:T(8,128)S(1)} all-gather(f32[128,128]{1,0:T(8,128)S(1)} %fusion), channel_id=2, replica_groups=mesh['rep'=8,'rows'=4] {'rep'}, dimensions={0}, use_global_device_ids=true | all-gather | bytes 589824 | tf_op jit(solution)/shard_map/all_gather | solution.py:50
  84.0 0.1 multiply_reduce_fusion
  84.2 0.7 broadcast_divide_fusion
  (2 shorter events, 0.0 us)
Async XLA Ops:
  6.5 39.6 %all-gather.3.cloned.1.call-start = ((), (), s32[]{:S(2)}) async-start(), calls=%async_computation | async-start | bytes 5242880 | tf_op jit(solution)/shard_map/all_gather | solution.py:47
Sparse Core Ops, SparseCore 0:
  8.9 37.1 all-gather.2

commit v2 on v0

--- a/solution.py
+++ b/solution.py
@@ -3,6 +3,11 @@
 import jax.numpy as jnp
 from jax import lax
 from jax.sharding import PartitionSpec as P
+
+
+def gather_over(block, axis, dim):
+    sent = jnp.stack([block] * lax.axis_size(axis))
+    return jnp.concatenate(lax.all_to_all(sent, axis, 0, 0), axis=dim)
 
 
 def pool_rows(ids, mask, piece, offset):
@@ -42,10 +47,7 @@
     group_rows = rows_dev * group_size
     group_base = lax.axis_index("rep") * group_rows
     partial_value = pool_rows(
-        history_ids,
-        history_mask,
-        lax.all_gather(item_table, "rows", axis=0, tiled=True),
-        group_base,
+        history_ids, history_mask, gather_over(item_table, "rows", 0), group_base
     )
     pooled = lax.psum(partial_value, "rep")
     return normalize(pooled)

time: 132 us -> 151 us (1.14)
  waiting for transfers between devices: 96.3 us -> 108 us
  starting transfers between devices: 0.04 us -> 5.01 us
  local copies, waits for them, and re-layouts: 0.3 us -> 4.04 us
  other arithmetic: 4.08 us -> 2.56 us
    all_to_all x0 -> x1, waiting for transfers between devices: none -> 37.6 us  [gather_over(): return jnp.concatenate(lax.all_to_all(sent, axis, 0, 0), axis=dim)]
    all_gather x1 -> x0, waiting for transfers between devices: 26.1 us -> none  [on_device(): lax.all_gather(item_table, 'rows', axis=0, tiled=True)]
    all_to_all x0 -> x1, starting transfers between devices: none -> 4.97 us  [gather_over(): return jnp.concatenate(lax.all_to_all(sent, axis, 0, 0), axis=dim)]
    another operation x0 -> x1, local copies, waits for them, and re-layouts: none -> 3.74 us  [gather_over(): sent = jnp.stack([block] * lax.axis_size(axis))]
  transfers between devices with their start and end apart: 2 -> 2, of which waited for: 2 -> 2; matrix products, arithmetic and copies ran while one was open for 10% -> 7% of each run, Pallas kernels for 0% -> 0%
where the time goes in v2:
time: 151 us
  waiting for transfers between devices  108 us (72%)
  matrix products  17.7 us (12%)
  between operations  13.5 us (9%)
  starting transfers between devices  5.01 us (3%)
  local copies, waits for them, and re-layouts  4.04 us (3%)
  other arithmetic  2.56 us (2%)
    psum x1, waiting for transfers between devices, on_device(): pooled = lax.psum(partial_value, 'rep')  70.5 us
    all_to_all x1, waiting for transfers between devices, gather_over(): return jnp.concatenate(lax.all_to_all(sent, axis, 0, 0), axis=dim)  37.6 us
    dot_general x1, matrix products, one_block(): jnp.einsum('blh,blo->bho', high_hot, low_hot, preferred_element_type=jnp....  10.8 us
    dot_general x1, matrix products, one_block(): return jnp.dot(counts, piece, preferred_element_type=jnp.float32)  6.88 us
    all_to_all x1, starting transfers between devices, gather_over(): return jnp.concatenate(lax.all_to_all(sent, axis, 0, 0), axis=dim)  4.97 us
    another operation x1, local copies, waits for them, and re-layouts, gather_over(): sent = jnp.stack([block] * lax.axis_size(axis))  3.74 us
  transfers between devices with their start and end apart: 2, of which 2 were waited for; matrix products, arithmetic and copies ran while one was open for 7% of the time, Pallas kernels for 0%

profile of v2, /device:TPU:0, one launch (start us, length us, event | category | flops | bytes accessed | tf_op | source)
XLA Modules:
  0.0 150.9 jit_solution(2778348524605024095)
XLA Ops:
  6.5 3.7 %stack.2 = bf16[4,4096,128]{2,1,0:T(8,128)(2,1)} broadcast(bf16[4096,128]{1,0:T(8,128)(2,1)} %param.3), dimensions={1,2} | broadcast | bytes 5242880 | tf_op jit(solution)/shard_map/stack | solution.py:9
  10.3 0.0 copy-start
  10.3 0.0 copy-start.1
  10.3 5.0 %all-to-all-start = ((bf16[4,4096,128]{2,1,0:T(8,128)(2,1)}), bf16[4,4096,128]{2,1,0:T(8,128)(2,1)}, u32[]{:S(2)}, u32[]{:S(2)}) async-start(bf16[4,4096,128]{2,1,0:T(8,128)(2,1)} %stack.2), calls=%async_computation | async-start | bytes 8388608 | tf_op jit(solution)/shard_map/all_to_all | solution.py:10
  15.3 0.0 all-reduce.2.cloned.1.call-start
  15.3 0.0 copy-done
  15.4 0.1 copy.5
  15.5 0.1 copy.4
  15.6 0.0 copy-done.1
  15.6 0.1 copy.6
  15.7 10.8 %fusion.6 = bf16[128,128,128]{2,1,0:T(8,128)(2,1)} fusion(s32[128,64]{1,0:T(8,128)S(1)} %copy.5, s32[128,64]{1,0:T(8,128)S(1)} %copy.4, pred[128,64]{1,0:T(8,128)(4,1)S(1)} %copy.6), kind=kOutput, calls=%fused_computation.7 | convolution fusion | flops 273678336 | bytes 4268032 | tf_op jit(solution)/shard_map/while/body/eval_jaxpr/blh,blo->bho/dot_general | solution.py:28
  26.5 37.6 %all-to-all-done = bf16[4,4096,128]{2,1,0:T(8,128)(2,1)} async-done(((bf16[4,4096,128]{2,1,0:T(8,128)(2,1)}), bf16[4,4096,128]{2,1,0:T(8,128)(2,1)}, u32[]{:S(2)}, u32[]{:S(2)}) %all-to-all-start) | async-done | bytes 4194336 | tf_op jit(solution)/shard_map/all_to_all | solution.py:10
  64.1 6.9 %fusion = f32[128,128]{1,0:T(8,128)} fusion(bf16[16384,128]{1,0:T(8,128)(2,1)} %bitcast, bf16[16,8,128,128]{3,2,1,0:T(8,128)(2,1)} %bitcast.6), kind=kOutput, calls=%fused_computation | convolution fusion | flops 536870912 | bytes 8454144 | tf_op jit(solution)/shard_map/while/body/eval_jaxpr/dot_general | solution.py:30
  71.0 0.0 all-reduce.2.cloned.1.call-update
  71.1 70.5 %all-reduce.2.cloned.1.call-done = f32[128,128]{1,0:T(8,128)} async-done(((f32[128,128]{1,0:T(8,128)}), f32[128,128]{1,0:T(8,128)}) %all-reduce.2.cloned.1.call-update) | async-done | bytes 65552 | tf_op jit(solution)/shard_map/psum | solution.py:52
  141.5 0.9 multiply_reduce_fusion
  142.5 1.6 %broadcast_divide_fusion = f32[128,128]{1,0:T(8,128)} fusion(f32[128,128]{1,0:T(8,128)} %all-reduce.2.cloned.1.call-done, f32[128]{0:T(128)S(1)} %add_sqrt_fusion), kind=kLoop, calls=%fused_computation.17 | loop fusion | flops 16384 | bytes 131584 | tf_op jit(solution)/shard_map/div | solution.py:41
  (3 shorter events, 0.1 us)
Async XLA Ops:
  10.3 5.0 %copy-start = (s32[128,64]{0,1:T(8,128)S(1)}, s32[128,64]{0,1:T(8,128)}, u32[]{:S(2)}) copy-start(s32[128,64]{0,1:T(8,128)} %param.4) | copy-start | bytes 98308
  10.3 5.3 %copy-start.1 = (s32[128,64]{0,1:T(8,128)S(1)}, s32[128,64]{0,1:T(8,128)}, u32[]{:S(2)}) copy-start(s32[128,64]{0,1:T(8,128)} %param.5) | copy-start | bytes 98308
  10.3 53.9 %all-to-all-start = ((bf16[4,4096,128]{2,1,0:T(8,128)(2,1)}), bf16[4,4096,128]{2,1,0:T(8,128)(2,1)}, u32[]{:S(2)}, u32[]{:S(2)}) async-start(bf16[4,4096,128]{2,1,0:T(8,128)(2,1)} %stack.2), calls=%async_computation | async-start | bytes 8388608 | tf_op jit(solution)/shard_map/all_to_all | solution.py:10
  15.3 126.3 %all-reduce.2.cloned.1.call-start = ((), (), s32[]{:S(2)}) async-start(), calls=%async_computation.1 | async-start | bytes 131072 | tf_op jit(solution)/shard_map/psum | solution.py:52
Sparse Core Ops, SparseCore 0:
  71.2 70.3 all-reduce.1
